TPU v7x, 32 devices: a whole 2x2x4 slice. The times are simulated.
32 devices in a mesh: gx: 4 (over x, core), gy: 4 (over z), gz: 2 (over y).
Axes of the slice: x: 2, y: 2, z: 4, core: 2. Of those that a mesh axis runs over, the one named last changes fastest.
Arguments:
- amplitudes: bfloat16 [2, 16384, 2048], P(None, ('gx', 'gy', 'gz')), may hold values from -6 to 6
- pauli_x: int32 [200], replicated, may hold values from 0 to 2047, as said below
- pauli_z: int32 [200], replicated, may hold values from 0 to 2047
- pauli_phase: int32 [200], replicated, may hold values from 0 to 3
Outputs:
- density_real: float32 [2048, 2048], P(('gx', 'gy', 'gz'))
- density_imag: float32 [2048, 2048], P(('gx', 'gy', 'gz'))
- expectations: float32 [2, 200], replicated
Inputs may be any that keep to these rules, and one draw needn't show every extreme that they name: Bit q of the mask acts on kept qubit q (the bit of weight 2^q of the last index); pauli_x and pauli_z of a term are never both zero.
All inputs are finite; a program needn't handle non-finite values.
Results may differ from a plain program's by a relative error of at most 0.0003.
Values sent between devices are 32-bit elements; how exact they have to be, the bound alone decides.
A program may use at most 192 MiB of HBM per device.

v0:
```python
import jax
import jax.numpy as jnp
from jax import lax
from jax.sharding import PartitionSpec as P

QUBITS = 11


def parity_sign(values, masks):
    anded = jnp.bitwise_and(values, masks)
    counted = jnp.zeros_like(anded)
    for bit_index in range(QUBITS):
        counted = counted + jnp.bitwise_and(jnp.right_shift(anded, bit_index), 1)
    return (1 - 2 * jnp.bitwise_and(counted, 1)).astype(jnp.float32)


def phase_parts(pauli_phase):
    phase_real = jnp.where(pauli_phase == 0, 1.0, jnp.where(pauli_phase == 2, -1.0, 0.0)).astype(
        jnp.float32
    )
    phase_imag = jnp.where(pauli_phase == 1, 1.0, jnp.where(pauli_phase == 3, -1.0, 0.0)).astype(
        jnp.float32
    )
    return (phase_real, phase_imag)


def on_device(amplitudes, pauli_x, pauli_z, pauli_phase):
    real_part = amplitudes[0]
    imag_part = amplitudes[1]
    order = real_part.shape[1]
    stacked = jnp.concatenate([real_part, imag_part], 0)
    crossed = jnp.concatenate([imag_part, jnp.negative(real_part)], 0)
    dims = (((0,), (0,)), ((), ()))
    devices = lax.axis_size("gx") * lax.axis_size("gy") * lax.axis_size("gz")
    own_count = order // devices
    real_rows = lax.dot_general(stacked, stacked, dims, preferred_element_type=jnp.float32)
    imag_rows = lax.dot_general(crossed, stacked, dims, preferred_element_type=jnp.float32)
    by_gx = lax.psum_scatter(
        jnp.concatenate([real_rows, imag_rows], 1), "gx", scatter_dimension=0, tiled=True
    )
    by_gy = lax.psum_scatter(by_gx, "gy", scatter_dimension=0, tiled=True)
    summed = lax.psum_scatter(by_gy, "gz", scatter_dimension=0, tiled=True)
    total_cols = amplitudes.shape[1] * devices
    density = summed / total_cols
    density_real = density[:, :order]
    density_imag = density[:, order:]
    first_row = lax.axis_index(("gx", "gy", "gz")) * own_count
    owned_rows = (first_row + jnp.arange(own_count, dtype=jnp.int32))[:, None]
    partner = jnp.bitwise_xor(owned_rows, pauli_x[None, :])
    picked_real = jnp.take_along_axis(density_real, partner, axis=1)
    picked_imag = jnp.take_along_axis(density_imag, partner, axis=1)
    signs = parity_sign(owned_rows, pauli_z[None, :])
    phase_real, phase_imag = phase_parts(pauli_phase)
    sum_real = jnp.sum(signs * picked_real, axis=0)
    sum_imag = jnp.sum(signs * picked_imag, axis=0)
    local_real = phase_real * sum_real - phase_imag * sum_imag
    local_imag = phase_real * sum_imag + phase_imag * sum_real
    expectations = lax.psum(jnp.stack([local_real, local_imag], 0), ("gx", "gy", "gz"))
    return (density_real, density_imag, expectations)


def solution(mesh):
    return jax.shard_map(
        on_device,
        mesh=mesh,
        in_specs=(P(None, ("gx", "gy", "gz"), None), P(), P(), P()),
        out_specs=(P(("gx", "gy", "gz"), None), P(("gx", "gy", "gz"), None), P()),
        check_vma=False,
    )
```

profile of v0, /device:TPU:0, one launch (start us, length us, event | category | flops | bytes accessed | tf_op | source)
XLA Modules:
  0.0 697.3 jit_solution(880764273149815197)
XLA Ops:
  7.2 0.0 reduce-scatter.6.cloned.1.call-start
  7.2 0.0 copy-start
  7.2 4.9 slice_bitcast_fusion.1
  12.1 0.0 copy-done
  12.1 0.1 fusion.37
  12.2 12.8 %fusion.4 = f32[2048,2048]{0,1:T(8,128)S(1)} fusion(bf16[512,2048]{1,0:T(8,128)(2,1)} %get-tuple-element.19, bf16[512,2048]{1,0:T(8,128)(2,1)} %get-tuple-element.18), kind=kOutput, calls=%fused_computation.8 | convolution fusion | flops 8598323200 | bytes 20971520 | tf_op jit(solution)/shard_map/dot_general | solution.py:36
  25.1 14.8 %fusion = f32[2048,2048]{0,1:T(8,128)} fusion(bf16[512,2048]{1,0:T(8,128)(2,1)S(1)} %fusion.37, bf16[512,2048]{1,0:T(8,128)(2,1)} %get-tuple-element.19, bf16[512,2048]{1,0:T(8,128)(2,1)} %get-tuple-element.18), kind=kOutput, calls=%fused_computation.4 | convolution fusion | flops 8606711808 | bytes 23068672 | tf_op jit(solution)/shard_map/dot_general | solution.py:37
  39.8 18.9 %pad_maximum_fusion = f32[2048,4096]{0,1:T(8,128)} fusion(f32[2048,2048]{0,1:T(8,128)} %fusion, f32[2048,2048]{0,1:T(8,128)S(1)} %fusion.4), kind=kLoop, calls=%fused_computation.2 | loop fusion | flops 8388608 | bytes 67108864 | tf_op jit(solution)/shard_map/concatenate | solution.py:39
  58.7 0.0 reduce-scatter.6.cloned.1.call-update
  58.7 0.0 reduce-scatter.8.cloned.1.call-start
  58.8 235.0 %reduce-scatter.6.cloned.1.call-done = f32[512,4096]{0,1:T(8,128)} async-done(((f32[2048,4096]{0,1:T(8,128)}), f32[512,4096]{0,1:T(8,128)}) %reduce-scatter.6.cloned.1.call-update) | async-done | bytes 8388624 | tf_op jit(solution)/shard_map/reduce_scatter | solution.py:38
  293.8 0.0 copy-start.1
  293.8 0.0 reduce-scatter.8.cloned.1.call-update
  293.8 0.2 reduce-scatter.10.cloned.1.call-start
  294.0 146.8 %reduce-scatter.8.cloned.1.call-done = f32[128,4096]{0,1:T(8,128)} async-done(((f32[512,4096]{0,1:T(8,128)}), f32[128,4096]{0,1:T(8,128)}) %reduce-scatter.8.cloned.1.call-update) | async-done | bytes 2097168 | tf_op jit(solution)/shard_map/reduce_scatter | solution.py:41
  440.8 2.9 copy.15
  443.6 0.0 reduce-scatter.10.cloned.1.call-update
  443.7 0.0 copy-done.1
  443.7 0.1 bitcast_or_fusion
  443.8 0.1 reshape.44
  443.9 32.4 %reduce-scatter.10.cloned.1.call-done = f32[64,4096]{1,0:T(8,128)} async-done(((f32[128,4096]{1,0:T(8,128)}), f32[64,4096]{1,0:T(8,128)}) %reduce-scatter.10.cloned.1.call-update) | async-done | bytes 1048592
  476.3 1.8 copy.16
  478.2 0.1 broadcast_multiply_fusion
  478.3 0.1 fusion.38
  478.5 1.1 copy.13
  479.6 85.1 %gather_fusion = f32[12800]{0:T(1024)S(1)} fusion(f32[64,2048]{0,1:T(8,128)S(1)} %get-tuple-element.21, s32[12800]{0:T(1024)S(1)} %reshape.44), kind=kCustom, calls=%fused_computation.clone | custom fusion | bytes 204800 | tf_op jit(solution)/shard_map/jit(take_along_axis)/gather | solution.py:50
  564.7 0.0 copy-start.2
  564.7 0.0 copy-start.3
  564.7 85.1 %gather_fusion.1 = f32[12800]{0:T(1024)S(1)} fusion(f32[64,2048]{0,1:T(8,128)S(1)} %get-tuple-element.20, s32[12800]{0:T(1024)S(1)} %reshape.44), kind=kCustom, calls=%fused_computation.1.clone | custom fusion | bytes 204800 | tf_op jit(solution)/shard_map/jit(take_along_axis)/gather | solution.py:51
  649.8 1.1 copy.14
  650.9 0.1 reshape.47
  651.1 0.1 reshape.52
  651.2 0.0 copy-done.2
  651.2 0.2 fusion.30
  651.4 0.0 copy-done.3
  651.4 39.3 %psum.7 = f32[2,200]{1,0:T(2,128)} all-reduce(f32[2,200]{1,0:T(2,128)S(1)} %pad_maximum_fusion.4), channel_id=1, replica_groups=mesh['gx'=4,'gy'=4,'gz'=2] {'gx','gy','gz'}, use_global_device_ids=true, to_apply=%region_5.7 | all-reduce | flops 400 | bytes 3200 | tf_op jit(solution)/shard_map/psum | solution.py:58
  (3 shorter events, 0.0 us)
Async XLA Ops:
  7.2 286.6 %reduce-scatter.6.cloned.1.call-start = ((), (), s32[]{:S(2)}) async-start(), calls=%async_computation.3 | async-start | bytes 41943040 | tf_op jit(solution)/shard_map/reduce_scatter | solution.py:38
  7.2 4.9 copy-start
  58.7 382.0 %reduce-scatter.8.cloned.1.call-start = ((), (), s32[]{:S(2)}) async-start(), calls=%async_computation.4 | async-start | bytes 10485760 | tf_op jit(solution)/shard_map/reduce_scatter | solution.py:41
  293.8 149.9 %copy-start.1 = (s32[200]{0:T(256)S(1)}, s32[200]{0:T(256)}, u32[]{:S(2)}) copy-start(s32[200]{0:T(256)} %param.7) | copy-start | bytes 2404
  293.8 182.6 %reduce-scatter.10.cloned.1.call-start = ((), (), s32[]{:S(2)}) async-start(), calls=%async_computation.5 | async-start | bytes 3145728
  564.7 86.5 %copy-start.2 = (s32[200]{0:T(256)S(1)}, s32[200]{0:T(256)}, u32[]{:S(2)}) copy-start(s32[200]{0:T(256)} %param.8) | copy-start | bytes 2404
  564.7 86.7 %copy-start.3 = (s32[200]{0:T(256)S(1)}, s32[200]{0:T(256)}, u32[]{:S(2)}) copy-start(s32[200]{0:T(256)} %param.9) | copy-start | bytes 2404
Sparse Core Ops, SparseCore 0:
  58.9 234.8 reduce-scatter.5
  296.1 144.6 reduce-scatter.7
  443.8 32.5 reduce-scatter.9
where the time goes:
time: 698 us; the launch traced here: 697 us
  waiting for transfers between devices  414 us (59%)
  local copies, waits for them, and re-layouts  183 us (26%)
  blocking collectives  39.3 us (6%)
  matrix products  27.6 us (4%)
  other arithmetic  19.5 us (3%)
  between operations  13.9 us (2%)
    reduce_scatter x1, waiting for transfers between devices, on_device(): lax.psum_scatter(jnp.concatenate([real_rows, imag_rows], 1), 'gx', scatte...  235 us
    reduce_scatter x1, waiting for transfers between devices, on_device(): by_gy = lax.psum_scatter(by_gx, 'gy', scatter_dimension=0, tiled=True)  147 us
    gather x3, local copies, waits for them, and re-layouts, on_device(): picked_real = jnp.take_along_axis(density_real, partner, axis=1)  85.3 us
    gather x2, local copies, waits for them, and re-layouts, on_device(): picked_imag = jnp.take_along_axis(density_imag, partner, axis=1)  85.2 us
    psum x1, blocking collectives, on_device(): lax.psum(jnp.stack([local_real, local_imag], 0), ('gx', 'gy', 'gz'))  39.3 us
    unnamed x4, waiting for transfers between devices  32.5 us
    concatenate x1, other arithmetic, on_device(): jnp.concatenate([real_rows, imag_rows], 1)  18.9 us
    dot_general x1, matrix products, on_device(): lax.dot_general(crossed, stacked, dims, preferred_element_type=jnp.float32)  14.8 us
  transfers between devices with their start and end apart: 3, of which 3 were waited for; matrix products, arithmetic and copies ran while one was open for 0% of the time, Pallas kernels for 0%

commit v1 on v0

v1 whole, which is shorter than its diff:
```python
import functools

import jax
import jax.numpy as jnp
from jax import lax
from jax.experimental import pallas as pl
from jax.experimental.pallas import tpu as pltpu
from jax.sharding import PartitionSpec as P

AXES = ("gx", "gy", "gz")
LANES = 128
MESH = pl.DeviceIdType.MESH


def log2(value):
    return value.bit_length() - 1


def flat_index(sizes):
    return (lax.axis_index("gx") * sizes[1] + lax.axis_index("gy")) * sizes[2] + lax.axis_index("gz")


def coords(flat, sizes):
    return (flat // (sizes[1] * sizes[2]), (flat // sizes[2]) % sizes[1], flat % sizes[2])


def flip(bit, by):
    return bit + by - 2 * bit * by


def stage_order(sizes):
    zs = log2(sizes[2])
    ys = log2(sizes[1])
    xs = log2(sizes[0])
    low = [zs + ys]
    rest_x = [zs + ys + t for t in range(xs - 1, 0, -1)]
    rest_z = list(range(zs - 1, -1, -1))
    rest_y = [zs + t for t in range(ys - 1, -1, -1)]
    return low + rest_x + rest_z + rest_y


def gram_kernel(sizes, total_cols, amp, kept, mirrored, ext, part, land, turned, came, load_sem, send_sem, recv_sem, msend, mrecv):
    n = sizes[0] * sizes[1] * sizes[2]
    nbits = log2(n)
    depth = amp.shape[1]
    order = amp.shape[2]
    own = order // n
    block = max(own, LANES)
    q = block // own
    blocks = order // block
    width = (blocks // 2 + 1) * block
    me = flat_index(sizes)
    bits = [(me // (1 << p)) % 2 for p in range(nbits)]
    stages = stage_order(sizes)
    half = bits[stages[0]]

    def loads():
        out = []
        for part_index in range(2):
            rows = pl.ds(part_index * depth, depth)
            out.append(pltpu.make_async_copy(amp.at[part_index], ext.at[rows, pl.ds(0, order)], load_sem.at[2 * part_index]))
            out.append(
                pltpu.make_async_copy(
                    amp.at[part_index, :, pl.ds(0, width - block)],
                    ext.at[rows, pl.ds(order, width - block)],
                    load_sem.at[2 * part_index + 1],
                )
            )
        return out

    for copy in loads():
        copy.start()

    def flips_of(v):
        by_stage = [(v >> (nbits - 1 - s)) & 1 for s in range(nbits)]
        flips = [0] * nbits
        for s, p in enumerate(stages):
            flips[p] = by_stage[s]
        if by_stage[1] != by_stage[2]:
            first, second = stages[1], stages[2]
            flips[first] = by_stage[1] * (1 - half) + by_stage[2] * half
            flips[second] = by_stage[2] * (1 - half) + by_stage[1] * half
        return flips

    def place(flips):
        return sum((1 << p) * flip(bits[p], flips[p]) for p in range(nbits))

    def name(flips):
        return sum((1 << p) * flips[p] for p in range(nbits))

    def message(where, ident, target):
        return pltpu.make_async_remote_copy(
            src_ref=part.at[where],
            dst_ref=land.at[ident],
            send_sem=send_sem.at[ident],
            recv_sem=recv_sem.at[ident],
            device_id=coords(target, sizes),
            device_id_type=MESH,
        )

    partner = [place(flips_of(1 << (nbits - 1 - s))) for s in range(nbits)]
    lowbits = log2(q)
    high = [p for p in stages[1:] if p >= lowbits]

    def row_block(u):
        flips = [0] * nbits
        flips[stages[0]] = 1 - u % 2
        for j, p in enumerate(high):
            flips[p] = 1 - (u // (1 << (len(high) - j))) % 2
        return flips

    for copy in loads():
        copy.wait()

    def compute(u, _):
        @pl.when(u % 2 == 1)
        def _():
            for g in range(q):
                flips = row_block(u - 1)
                for p in range(lowbits):
                    flips[p] = (g >> p) & 1
                message(place(flips), name(flips), partner[0]).start()

        flips = row_block(u)
        first = sum((1 << p) * flip(bits[p], flips[p]) for p in range(lowbits, nbits))
        start = pl.multiple_of(first * own, block)
        lhs = ext[:, pl.ds(start, block)]
        crossed = jnp.concatenate([lhs[depth:], -lhs[:depth]], 0)
        both = jnp.concatenate([lhs, crossed], 1)
        rhs = ext[:, pl.ds(start, width)]
        rows = lax.dot_general(both, rhs, (((0,), (0,)), ((), ())), preferred_element_type=jnp.float32)
        for sub in range(q):
            part[first + sub, :, 0:width] = rows[sub * own : (sub + 1) * own]
            part[first + sub, :, width : 2 * width] = rows[block + sub * own : block + (sub + 1) * own]
        return 0

    lax.fori_loop(0, blocks, compute, 0)

    def gather_in(v, upto):
        where = place(flips_of(v))
        names = [name(flips_of(v | (1 << (nbits - 1 - t)))) for t in range(upto)]
        for ident in names:
            message(where, ident, partner[0]).wait_recv()
        for r in range(0, own, 8):
            rows = pl.ds(r, 8)
            total = part[where, rows, :]
            for ident in names:
                total = total + land[ident, rows, :]
            part[where, rows, :] = total
        return where

    for s in range(1, nbits):
        top = 1 << (nbits - 1 - s)
        for w in range(top - 1, -1, -1):
            v = top + w
            where = gather_in(v, s)
            message(where, name(flips_of(v)), partner[s]).start()

    gather_in(0, nbits)
    for r in range(0, own, 8):
        rows = pl.ds(r, 8)
        kept[rows, :] = part[me, rows, :] / total_cols

    mine = me // q
    sub_me = me % q

    def mirror(k, sub):
        target = ((mine + k) % blocks) * q + sub
        return pltpu.make_async_remote_copy(
            src_ref=turned.at[k - 1, pl.ds(sub * own, own)],
            dst_ref=came.at[(k - 1) * q + sub_me],
            send_sem=msend.at[(k - 1) * q + sub],
            recv_sem=mrecv.at[(k - 1) * q + sub_me],
            device_id=coords(target, sizes),
            device_id_type=MESH,
        )

    for k in range(1, blocks // 2):
        cols = kept[:, k * block : (k + 1) * block]
        more = kept[:, width + k * block : width + (k + 1) * block]
        turned[k - 1] = jnp.concatenate([cols, more], 0).T
    for k in range(1, blocks // 2):
        for sub in range(q):
            mirror(k, sub).start()
    for k in range(1, blocks // 2):
        for sub in range(q):
            slot = (k - 1) * q + sub
            pltpu.make_async_remote_copy(
                src_ref=turned.at[k - 1, pl.ds(sub * own, own)],
                dst_ref=came.at[slot],
                send_sem=msend.at[slot],
                recv_sem=mrecv.at[slot],
                device_id=coords(((mine + k) % blocks) * q + sub, sizes),
                device_id_type=MESH,
            ).wait()
            mirrored[slot] = came[slot]

    def drain(ident, _):
        message(0, ident, partner[0]).wait_send()
        return 0

    lax.fori_loop(1, n, drain, 0)


def finish_kernel(sizes, kept, mirrored, px, pz, phase, real, imag, expect):
    n = sizes[0] * sizes[1] * sizes[2]
    own, order = real.shape
    block = max(own, LANES)
    q = block // own
    blocks = order // block
    width = (blocks // 2 + 1) * block
    me = flat_index(sizes)
    mine = me // q

    def columns(k):
        return pl.ds(pl.multiple_of(((mine + k + blocks) % blocks) * block, block), block)

    for k in range(blocks // 2 + 1):
        real[:, columns(k)] = kept[:, k * block : (k + 1) * block]
        imag[:, columns(k)] = kept[:, width + k * block : width + (k + 1) * block]
    for k in range(1, blocks // 2):
        tiles = [mirrored[(k - 1) * q + sub] for sub in range(q)]
        real[:, columns(-k)] = jnp.concatenate([t[:, :own] for t in tiles], 1)
        imag[:, columns(-k)] = -jnp.concatenate([t[:, own:] for t in tiles], 1)

    terms = px.shape[0]
    base = me * own
    ids = base + lax.broadcasted_iota(jnp.int32, (terms, own), 1)
    anded = jnp.bitwise_and(ids, pz[...])
    shift = 16
    while shift >= 1:
        anded = jnp.bitwise_xor(anded, jnp.right_shift(anded, shift))
        shift //= 2
    signs = (1 - 2 * jnp.bitwise_and(anded, 1)).astype(jnp.float32)
    wanted = jnp.bitwise_xor(px[...], base)
    row = lax.broadcasted_iota(jnp.int32, (own, block), 0)
    lane = lax.broadcasted_iota(jnp.int32, (own, block), 1)
    lane_terms = lax.broadcasted_iota(jnp.int32, (terms, block), 1)

    def picked(ref, tile):
        values = ref[:, pl.ds(pl.multiple_of(tile * block, block), block)]
        for p in range(log2(own)):
            step = 1 << p
            swapped = jnp.where(
                jnp.bitwise_and(lane, step) != 0,
                pltpu.roll(values, step, 1),
                pltpu.roll(values, block - step, 1),
            )
            values = jnp.where(jnp.bitwise_and(row, step) != 0, swapped, values)
        sums = lax.dot_general(
            signs, values, (((1,), (0,)), ((), ())), precision=lax.Precision.HIGHEST, preferred_element_type=jnp.float32
        )
        return jnp.where(lane_terms + tile * block == wanted, sums, 0.0)

    def body(tile, carry):
        return carry[0] + picked(real, tile), carry[1] + picked(imag, tile)

    zeros = jnp.zeros((terms, block), jnp.float32)
    sum_real, sum_imag = lax.fori_loop(0, blocks, body, (zeros, zeros))
    sum_real = jnp.sum(sum_real, axis=1, keepdims=True)
    sum_imag = jnp.sum(sum_imag, axis=1, keepdims=True)
    turn = phase[...]
    phase_real = jnp.where(turn == 0, 1.0, jnp.where(turn == 2, -1.0, 0.0))
    phase_imag = jnp.where(turn == 1, 1.0, jnp.where(turn == 3, -1.0, 0.0))
    expect[:, 0:1] = phase_real * sum_real - phase_imag * sum_imag
    expect[:, 1:2] = phase_real * sum_imag + phase_imag * sum_real


def on_device(sizes, amplitudes, pauli_x, pauli_z, pauli_phase):
    n = sizes[0] * sizes[1] * sizes[2]
    _, depth, order = amplitudes.shape
    own = order // n
    block = max(own, LANES)
    q = block // own
    blocks = order // block
    width = (blocks // 2 + 1) * block
    slots = (blocks // 2 - 1) * q
    vmem = pl.BlockSpec(memory_space=pltpu.VMEM)
    kept, mirrored = pl.pallas_call(
        functools.partial(gram_kernel, sizes, float(depth * n)),
        out_shape=(
            jax.ShapeDtypeStruct((own, 2 * width), jnp.float32),
            jax.ShapeDtypeStruct((slots, own, 2 * own), jnp.float32),
        ),
        in_specs=[pl.BlockSpec(memory_space=pl.ANY)],
        out_specs=(vmem, vmem),
        scratch_shapes=[
            pltpu.VMEM((2 * depth, order + width - block), jnp.bfloat16),
            pltpu.VMEM((n, own, 2 * width), jnp.float32),
            pltpu.VMEM((n, own, 2 * width), jnp.float32),
            pltpu.VMEM((blocks // 2 - 1, block, 2 * own), jnp.float32),
            pltpu.VMEM((slots, own, 2 * own), jnp.float32),
            pltpu.SemaphoreType.DMA((4,)),
            pltpu.SemaphoreType.DMA((n,)),
            pltpu.SemaphoreType.DMA((n,)),
            pltpu.SemaphoreType.DMA((slots,)),
            pltpu.SemaphoreType.DMA((slots,)),
        ],
        compiler_params=pltpu.CompilerParams(has_side_effects=True, vmem_limit_bytes=60 << 20),
    )(amplitudes)
    terms = pauli_x.shape[0]
    real, imag, expect = pl.pallas_call(
        functools.partial(finish_kernel, sizes),
        out_shape=(
            jax.ShapeDtypeStruct((own, order), jnp.float32),
            jax.ShapeDtypeStruct((own, order), jnp.float32),
            jax.ShapeDtypeStruct((terms, 2), jnp.float32),
        ),
        in_specs=[vmem] * 5,
        out_specs=(vmem,) * 3,
    )(kept, mirrored, pauli_x[:, None], pauli_z[:, None], pauli_phase[:, None])
    return real, imag, lax.psum(expect.T, AXES)


def solution(mesh):
    sizes = tuple(mesh.shape[axis] for axis in AXES)
    return jax.shard_map(
        functools.partial(on_device, sizes),
        mesh=mesh,
        in_specs=(P(None, AXES, None), P(), P(), P()),
        out_specs=(P(AXES, None), P(AXES, None), P()),
        check_vma=False,
    )
```

time: 698 us -> 215 us (0.31)
  waiting for transfers between devices: 414 us -> 0 us
  local copies, waits for them, and re-layouts: 183 us -> 4.98 us
  Pallas kernels: 0 us -> 170 us
  matrix products: 27.6 us -> 0 us
  other arithmetic: 19.5 us -> 0 us
  between operations: 13.9 us -> 0.65 us
    reduce_scatter x2 -> x0, waiting for transfers between devices: 382 us -> none  [the longest x1 235 us: on_device(): lax.psum_scatter(jnp.concatenate([real_rows, imag_rows], 1), 'gx', scatte...]
    gather x5 -> x0, local copies, waits for them, and re-layouts: 171 us -> none  [the longest x3 85.3 us: on_device(): picked_real = jnp.take_along_axis(density_real, partner, axis=1)]
    pallas_call x0 -> x2, Pallas kernels: none -> 170 us  [the longest x1 153 us: on_device(): pl.pallas_call(functools.partial(gram_kernel, sizes, float(depth * n)), o...]
    unnamed x4 -> x0, waiting for transfers between devices: 32.5 us -> none
    dot_general x2 -> x0, matrix products: 27.6 us -> none  [the longest x1 14.8 us: on_device(): lax.dot_general(crossed, stacked, dims, preferred_element_type=jnp.float32)]
    concatenate x1 -> x0, other arithmetic: 18.9 us -> none  [on_device(): jnp.concatenate([real_rows, imag_rows], 1)]
  transfers between devices with their start and end apart: 3 -> 0, of which waited for: 3 -> 0; matrix products, arithmetic and copies ran while one was open for 0% -> 0% of each run, Pallas kernels for 0% -> 0%
where the time goes in v1:
time: 215 us
  Pallas kernels  170 us (79%)
  blocking collectives  39.7 us (18%)
  local copies, waits for them, and re-layouts  4.98 us (2%)
    pallas_call x1, Pallas kernels, on_device(): pl.pallas_call(functools.partial(gram_kernel, sizes, float(depth * n)), o...  153 us
    psum x1, blocking collectives, on_device(): return (real, imag, lax.psum(expect.T, AXES))  39.7 us
    pallas_call x1, Pallas kernels, on_device(): pl.pallas_call(functools.partial(finish_kernel, sizes), out_shape=(jax.Sh...  16.6 us

profile of v1, /device:TPU:0, one launch (start us, length us, event | category | flops | bytes accessed | tf_op | source)
XLA Modules:
  0.0 215.1 jit_solution(18112111835885231365)
XLA Ops:
  0.6 1.4 copy.8.px
  2.1 1.4 copy.9.pz
  3.5 1.4 copy.10.phase
  5.0 153.1 %shard_map.67 = (f32[64,2304]{1,0:T(8,128)}, f32[14,64,128]{2,1,0:T(8,128)}) custom-call(bf16[2,512,2048]{2,1,0:T(8,128)(2,1)} %amp.1), custom_call_target="tpu_custom_call" | custom-call | tf_op jit(solution)/shard_map/pallas_call | solution.py:279
  158.0 16.6 %shard_map.68 = (f32[64,2048]{1,0:T(8,128)}, f32[64,2048]{1,0:T(8,128)}, f32[200,2]{1,0:T(8,128)}) custom-call(f32[64,2304]{1,0:T(8,128)} %get-tuple-element.8.kept, f32[14,64,128]{2,1,0:T(8,128)} %get-tuple-element.9.mirrored, s32[200,1]{1,0:T(8,128)} %copy.8.px, s32[200,1]{1,0:T(8,128)} %copy.9.pz, s32[200,1]{1,0:T(8,128)} %copy.10.phase), custom_call_target="tpu_custom_call" | custom-call | tf_op jit(solution)/shard_map/pallas_call | solution.py:302
  174.6 39.7 %psum.7 = f32[2,200]{0,1:T(8,128)S(1)} all-reduce(f32[2,200]{0,1:T(8,128)} %bitcast.4), channel_id=1, replica_groups=mesh['gx'=4,'gy'=4,'gz'=2] {'gx','gy','gz'}, use_global_device_ids=true, to_apply=%region_0.0 | all-reduce | flops 400 | bytes 3200 | tf_op jit(solution)/shard_map/psum | solution.py:312
  214.4 0.7 copy.11

commit v2 on v1

--- a/solution.py
+++ b/solution.py
@@ -32,14 +32,26 @@
     zs = log2(sizes[2])
     ys = log2(sizes[1])
     xs = log2(sizes[0])
-    low = [zs + ys]
     rest_x = [zs + ys + t for t in range(xs - 1, 0, -1)]
+    rest_y = [zs + t for t in range(ys)]
     rest_z = list(range(zs - 1, -1, -1))
-    rest_y = [zs + t for t in range(ys - 1, -1, -1)]
-    return low + rest_x + rest_z + rest_y
-
-
-def gram_kernel(sizes, total_cols, amp, kept, mirrored, ext, part, land, turned, came, load_sem, send_sem, recv_sem, msend, mrecv):
+    order = [zs + ys] + rest_x + rest_y[:1] + rest_z + rest_y[1:]
+    trade = order.index(rest_z[0]) if rest_x and rest_z else 1
+    return order, trade
+
+
+def parity_sign(masked):
+    shift = 16
+    while shift >= 1:
+        masked = jnp.bitwise_xor(masked, jnp.right_shift(masked, shift))
+        shift //= 2
+    return (1 - 2 * jnp.bitwise_and(masked, 1)).astype(jnp.float32)
+
+
+def gram_kernel(
+    sizes, total_cols, amp, px, pz, phase, kept, mirrored, expect,
+    ext, part, land, turned, came, outbox, inbox, load_sem, send_sem, recv_sem, msend, mrecv, esend, erecv,
+):
     n = sizes[0] * sizes[1] * sizes[2]
     nbits = log2(n)
     depth = amp.shape[1]
@@ -51,7 +63,7 @@
     width = (blocks // 2 + 1) * block
     me = flat_index(sizes)
     bits = [(me // (1 << p)) % 2 for p in range(nbits)]
-    stages = stage_order(sizes)
+    stages, trade = stage_order(sizes)
     half = bits[stages[0]]
 
     def loads():
@@ -76,10 +88,9 @@
         flips = [0] * nbits
         for s, p in enumerate(stages):
             flips[p] = by_stage[s]
-        if by_stage[1] != by_stage[2]:
-            first, second = stages[1], stages[2]
-            flips[first] = by_stage[1] * (1 - half) + by_stage[2] * half
-            flips[second] = by_stage[2] * (1 - half) + by_stage[1] * half
+        if by_stage[1] != by_stage[trade]:
+            flips[stages[1]] = by_stage[1] * (1 - half) + by_stage[trade] * half
+            flips[stages[trade]] = by_stage[trade] * (1 - half) + by_stage[1] * half
         return flips
 
     def place(flips):
@@ -100,7 +111,7 @@
 
     partner = [place(flips_of(1 << (nbits - 1 - s))) for s in range(nbits)]
     lowbits = log2(q)
-    high = [p for p in stages[1:] if p >= lowbits]
+    high = [p for p in stages[-1:] + stages[1:-1] if p >= lowbits]
 
     def row_block(u):
         flips = [0] * nbits
@@ -112,14 +123,40 @@
     for copy in loads():
         copy.wait()
 
+    def add_in(where, names):
+        for ident in names:
+            message(where, ident, partner[0]).wait_recv()
+        for r in range(0, own, 8):
+            rows = pl.ds(r, 8)
+            total = part[where, rows, :]
+            for ident in names:
+                total = total + land[ident, rows, :]
+            part[where, rows, :] = total
+
+    def with_low(flips, g):
+        return [(g >> p) & 1 if p < lowbits else flips[p] for p in range(nbits)]
+
+    def second_stage(w):
+        for g in range(q):
+            flips = with_low(row_block(2 * w + 1), g)
+            goes = flips[stages[1]] * (1 - half) + flips[stages[trade]] * half
+
+            @pl.when(goes == 1)
+            def _():
+                where, ident = place(flips), name(flips)
+                add_in(where, [ident + (1 << stages[0])])
+                message(where, ident, partner[1]).start()
+
     def compute(u, _):
         @pl.when(u % 2 == 1)
         def _():
             for g in range(q):
-                flips = row_block(u - 1)
-                for p in range(lowbits):
-                    flips[p] = (g >> p) & 1
+                flips = with_low(row_block(u - 1), g)
                 message(place(flips), name(flips), partner[0]).start()
+
+        @pl.when((u % 2 == 1) & (u >= 5))
+        def _():
+            second_stage(u // 2 - 2)
 
         flips = row_block(u)
         first = sum((1 << p) * flip(bits[p], flips[p]) for p in range(lowbits, nbits))
@@ -136,25 +173,19 @@
 
     lax.fori_loop(0, blocks, compute, 0)
 
+    for w in range(max(blocks // 2 - 2, 0), blocks // 2):
+        second_stage(w)
+
     def gather_in(v, upto):
         where = place(flips_of(v))
-        names = [name(flips_of(v | (1 << (nbits - 1 - t)))) for t in range(upto)]
-        for ident in names:
-            message(where, ident, partner[0]).wait_recv()
-        for r in range(0, own, 8):
-            rows = pl.ds(r, 8)
-            total = part[where, rows, :]
-            for ident in names:
-                total = total + land[ident, rows, :]
-            part[where, rows, :] = total
+        add_in(where, [name(flips_of(v | (1 << (nbits - 1 - t)))) for t in range(upto)])
         return where
 
-    for s in range(1, nbits):
-        top = 1 << (nbits - 1 - s)
-        for w in range(top - 1, -1, -1):
-            v = top + w
-            where = gather_in(v, s)
-            message(where, name(flips_of(v)), partner[s]).start()
+    later = 1 << (nbits - 2)
+    for v in sorted(range(1, later), key=lambda v: (v % 2 == 0, -v)):
+        s = nbits - v.bit_length()
+        where = gather_in(v, s)
+        message(where, name(flips_of(v)), partner[s]).start()
 
     gather_in(0, nbits)
     for r in range(0, own, 8):
@@ -182,6 +213,86 @@
     for k in range(1, blocks // 2):
         for sub in range(q):
             mirror(k, sub).start()
+    terms = px.shape[1]
+    base = me * own
+    ids = base + lax.broadcasted_iota(jnp.int32, (own, terms), 0)
+    signs = parity_sign(jnp.bitwise_and(ids, pz[...]))
+    paired = parity_sign(jnp.bitwise_and(px[...], pz[...]))
+    wanted = jnp.bitwise_xor(px[...], base)
+    row = lax.broadcasted_iota(jnp.int32, (own, block), 0)
+    lane = lax.broadcasted_iota(jnp.int32, (own, block), 1)
+    lane_terms = lax.broadcasted_iota(jnp.int32, (block, terms), 0)
+
+    def picked(first, k):
+        values = kept[:, first + k * block : first + (k + 1) * block]
+        for p in range(log2(own)):
+            step = 1 << p
+            swapped = jnp.where(
+                jnp.bitwise_and(lane, step) != 0,
+                pltpu.roll(values, step, 1),
+                pltpu.roll(values, block - step, 1),
+            )
+            values = jnp.where(jnp.bitwise_and(row, step) != 0, swapped, values)
+        sums = lax.dot_general(
+            values, signs, (((0,), (0,)), ((), ())), precision=lax.Precision.HIGHEST, preferred_element_type=jnp.float32
+        )
+        chosen = jnp.where(lane_terms + ((mine + k) % blocks) * block == wanted, sums, 0.0)
+        return jnp.sum(chosen, axis=0, keepdims=True)
+
+    def row_sums(first, sign):
+        ends = picked(first, 0) + picked(first, blocks // 2)
+        inner = jnp.zeros_like(ends)
+        for k in range(1, blocks // 2):
+            inner = inner + picked(first, k)
+        return ends + inner * (1.0 + sign * paired)
+
+    sum_real = row_sums(0, 1.0)
+    sum_imag = row_sums(width, -1.0)
+    turn = phase[...]
+    phase_real = jnp.where(turn == 0, 1.0, jnp.where(turn == 2, -1.0, 0.0))
+    phase_imag = jnp.where(turn == 1, 1.0, jnp.where(turn == 3, -1.0, 0.0))
+    total = jnp.concatenate(
+        [phase_real * sum_real - phase_imag * sum_imag, phase_real * sum_imag + phase_imag * sum_real], 0
+    )
+    here = coords(me, sizes)
+    first_slot = 0
+    for axis in range(3):
+        size = sizes[axis]
+        at = here[axis]
+        outbox[axis] = total
+        inbox[first_slot + at] = total
+        copies = []
+        for d in range(1, size):
+            target = list(here)
+            target[axis] = (at + d) % size
+            copies.append(
+                pltpu.make_async_remote_copy(
+                    src_ref=outbox.at[axis],
+                    dst_ref=inbox.at[first_slot + at],
+                    send_sem=esend.at[first_slot + d],
+                    recv_sem=erecv.at[first_slot + at],
+                    device_id=tuple(target),
+                    device_id_type=MESH,
+                )
+            )
+        for copy in copies:
+            copy.start()
+        for d in range(1, size):
+            source = first_slot + (at + d) % size
+            pltpu.make_async_remote_copy(
+                src_ref=outbox.at[axis],
+                dst_ref=inbox.at[source],
+                send_sem=esend.at[first_slot + d],
+                recv_sem=erecv.at[source],
+                device_id=tuple(target),
+                device_id_type=MESH,
+            ).wait()
+        total = inbox[first_slot]
+        for j in range(1, size):
+            total = total + inbox[first_slot + j]
+        first_slot += size
+    expect[...] = total
+
     for k in range(1, blocks // 2):
         for sub in range(q):
             slot = (k - 1) * q + sub
@@ -202,7 +313,7 @@
     lax.fori_loop(1, n, drain, 0)
 
 
-def finish_kernel(sizes, kept, mirrored, px, pz, phase, real, imag, expect):
+def finish_kernel(sizes, kept, mirrored, real, imag):
     n = sizes[0] * sizes[1] * sizes[2]
     own, order = real.shape
     block = max(own, LANES)
@@ -222,48 +333,6 @@
         tiles = [mirrored[(k - 1) * q + sub] for sub in range(q)]
         real[:, columns(-k)] = jnp.concatenate([t[:, :own] for t in tiles], 1)
         imag[:, columns(-k)] = -jnp.concatenate([t[:, own:] for t in tiles], 1)
-
-    terms = px.shape[0]
-    base = me * own
-    ids = base + lax.broadcasted_iota(jnp.int32, (terms, own), 1)
-    anded = jnp.bitwise_and(ids, pz[...])
-    shift = 16
-    while shift >= 1:
-        anded = jnp.bitwise_xor(anded, jnp.right_shift(anded, shift))
-        shift //= 2
-    signs = (1 - 2 * jnp.bitwise_and(anded, 1)).astype(jnp.float32)
-    wanted = jnp.bitwise_xor(px[...], base)
-    row = lax.broadcasted_iota(jnp.int32, (own, block), 0)
-    lane = lax.broadcasted_iota(jnp.int32, (own, block), 1)
-    lane_terms = lax.broadcasted_iota(jnp.int32, (terms, block), 1)
-
-    def picked(ref, tile):
-        values = ref[:, pl.ds(pl.multiple_of(tile * block, block), block)]
-        for p in range(log2(own)):
-            step = 1 << p
-            swapped = jnp.where(
-                jnp.bitwise_and(lane, step) != 0,
-                pltpu.roll(values, step, 1),
-                pltpu.roll(values, block - step, 1),
-            )
-            values = jnp.where(jnp.bitwise_and(row, step) != 0, swapped, values)
-        sums = lax.dot_general(
-            signs, values, (((1,), (0,)), ((), ())), precision=lax.Precision.HIGHEST, preferred_element_type=jnp.float32
-        )
-        return jnp.where(lane_terms + tile * block == wanted, sums, 0.0)
-
-    def body(tile, carry):
-        return carry[0] + picked(real, tile), carry[1] + picked(imag, tile)
-
-    zeros = jnp.zeros((terms, block), jnp.float32)
-    sum_real, sum_imag = lax.fori_loop(0, blocks, body, (zeros, zeros))
-    sum_real = jnp.sum(sum_real, axis=1, keepdims=True)
-    sum_imag = jnp.sum(sum_imag, axis=1, keepdims=True)
-    turn = phase[...]
-    phase_real = jnp.where(turn == 0, 1.0, jnp.where(turn == 2, -1.0, 0.0))
-    phase_imag = jnp.where(turn == 1, 1.0, jnp.where(turn == 3, -1.0, 0.0))
-    expect[:, 0:1] = phase_real * sum_real - phase_imag * sum_imag
-    expect[:, 1:2] = phase_real * sum_imag + phase_imag * sum_real
 
 
 def on_device(sizes, amplitudes, pauli_x, pauli_z, pauli_phase):
@@ -276,40 +345,44 @@
     width = (blocks // 2 + 1) * block
     slots = (blocks // 2 - 1) * q
     vmem = pl.BlockSpec(memory_space=pltpu.VMEM)
-    kept, mirrored = pl.pallas_call(
+    terms = pauli_x.shape[0]
+    kept, mirrored, expect = pl.pallas_call(
         functools.partial(gram_kernel, sizes, float(depth * n)),
         out_shape=(
             jax.ShapeDtypeStruct((own, 2 * width), jnp.float32),
             jax.ShapeDtypeStruct((slots, own, 2 * own), jnp.float32),
+            jax.ShapeDtypeStruct((2, terms), jnp.float32),
         ),
-        in_specs=[pl.BlockSpec(memory_space=pl.ANY)],
-        out_specs=(vmem, vmem),
+        in_specs=[pl.BlockSpec(memory_space=pl.ANY), vmem, vmem, vmem],
+        out_specs=(vmem,) * 3,
         scratch_shapes=[
             pltpu.VMEM((2 * depth, order + width - block), jnp.bfloat16),
             pltpu.VMEM((n, own, 2 * width), jnp.float32),
             pltpu.VMEM((n, own, 2 * width), jnp.float32),
             pltpu.VMEM((blocks // 2 - 1, block, 2 * own), jnp.float32),
             pltpu.VMEM((slots, own, 2 * own), jnp.float32),
+            pltpu.VMEM((3, 2, terms), jnp.float32),
+            pltpu.VMEM((sum(sizes), 2, terms), jnp.float32),
             pltpu.SemaphoreType.DMA((4,)),
             pltpu.SemaphoreType.DMA((n,)),
             pltpu.SemaphoreType.DMA((n,)),
             pltpu.SemaphoreType.DMA((slots,)),
             pltpu.SemaphoreType.DMA((slots,)),
+            pltpu.SemaphoreType.DMA((sum(sizes),)),
+            pltpu.SemaphoreType.DMA((sum(sizes),)),
         ],
         compiler_params=pltpu.CompilerParams(has_side_effects=True, vmem_limit_bytes=60 << 20),
-    )(amplitudes)
-    terms = pauli_x.shape[0]
-    real, imag, expect = pl.pallas_call(
+    )(amplitudes, pauli_x[None], pauli_z[None], pauli_phase[None])
+    real, imag = pl.pallas_call(
         functools.partial(finish_kernel, sizes),
         out_shape=(
             jax.ShapeDtypeStruct((own, order), jnp.float32),
             jax.ShapeDtypeStruct((own, order), jnp.float32),
-            jax.ShapeDtypeStruct((terms, 2), jnp.float32),
         ),
-        in_specs=[vmem] * 5,
-        out_specs=(vmem,) * 3,
-    )(kept, mirrored, pauli_x[:, None], pauli_z[:, None], pauli_phase[:, None])
-    return real, imag, lax.psum(expect.T, AXES)
+        in_specs=[vmem] * 2,
+        out_specs=(vmem,) * 2,
+    )(kept, mirrored)
+    return real, imag, expect
 
 
 def solution(mesh):

time: 215 us -> 120 us (0.56)
  Pallas kernels: 170 us -> 118 us
  blocking collectives: 39.7 us -> 0 us
  local copies, waits for them, and re-layouts: 4.98 us -> 1.23 us
    psum x1 -> x0, blocking collectives: 39.7 us -> none  [on_device(): return (real, imag, lax.psum(expect.T, AXES))]
    pallas_call x1, Pallas kernels: 153 us -> 116 us  [on_device(): pl.pallas_call(functools.partial(gram_kernel, sizes, float(depth * n)), o...]
    pallas_call x1, Pallas kernels: 16.6 us -> 2.34 us  [on_device(): pl.pallas_call(functools.partial(finish_kernel, sizes), out_shape=(jax.Sh...]
    broadcast_in_dim x3 -> x0, local copies, waits for them, and re-layouts: 4.32 us -> none  [the longest x1 1.45 us: on_device(): pauli_x[:, None]]
where the time goes in v2:
time: 120 us
  Pallas kernels  118 us (98%)
  local copies, waits for them, and re-layouts  1.23 us (1%)
    pallas_call x1, Pallas kernels, on_device(): pl.pallas_call(functools.partial(gram_kernel, sizes, float(depth * n)), o...  116 us

profile of v2, /device:TPU:0, one launch (start us, length us, event | category | flops | bytes accessed | tf_op | source)
XLA Modules:
  0.0 120.2 jit_solution(1709864075322164159)
XLA Ops:
  0.6 116.0 %shard_map.67 = (f32[64,2304]{1,0:T(8,128)}, f32[14,64,128]{2,1,0:T(8,128)}, f32[2,200]{1,0:T(2,128)}) custom-call(bf16[2,512,2048]{2,1,0:T(8,128)(2,1)} %amp.1, s32[1,200]{1,0:T(1,128)} %bitcast.3, s32[1,200]{1,0:T(1,128)} %bitcast.4, s32[1,200]{1,0:T(1,128)} %bitcast.5), custom_call_target="tpu_custom_call" | custom-call | tf_op jit(solution)/shard_map/pallas_call | solution.py:349
  116.7 2.3 %shard_map.68 = (f32[64,2048]{1,0:T(8,128)}, f32[64,2048]{1,0:T(8,128)}) custom-call(f32[64,2304]{1,0:T(8,128)} %get-tuple-element.8.kept, f32[14,64,128]{2,1,0:T(8,128)} %get-tuple-element.9.mirrored), custom_call_target="tpu_custom_call" | custom-call | tf_op jit(solution)/shard_map/pallas_call | solution.py:376
  119.0 1.2 %copy.8 = f32[2,200]{1,0:T(2,128)} copy(f32[2,200]{1,0:T(2,128)} %get-tuple-element.18) | data formatting | bytes 3200
